TPU v7x, 256 devices: a whole 4x4x8 slice. The times are simulated.
256 devices in a mesh: expert: 64 (over z, y, core), dp: 4 (over x).
Axes of the slice: x: 4, y: 4, z: 8, core: 2. Of those that a mesh axis runs over, the one named last changes fastest.
Arguments:
- tokens: bfloat16 [16384, 2880], P(('expert', 'dp')), may hold values from -6 to 6
- expert_ids: int32 [16384, 4], P(('expert', 'dp')), may hold values from 0 to 63, all different within a row; in each aligned block of 64 rows (0 to 63, 64 to 127, ...) at most 6 rows name the same one
- gate_logits: float32 [16384, 4], P(('expert', 'dp')), may hold values from -3 to 3
- w_gate: bfloat16 [64, 2880, 1536], P('expert', None, 'dp'), may hold values from -0.109375 to 0.109375
- w_up: bfloat16 [64, 2880, 1536], P('expert', None, 'dp'), may hold values from -0.109375 to 0.109375
- w_down: bfloat16 [64, 1536, 2880], P('expert', 'dp'), may hold values from -0.15625 to 0.15625
Outputs:
- mixed: bfloat16 [16384, 2880], P(('expert', 'dp'))
Inputs may be any that keep to these rules, and one draw needn't show every extreme that they name: `expert_ids`: each row names 4 different experts. Among the 64 rows of one device no expert is named more than 6 times, and every expert is named somewhere.
All inputs are finite; a program needn't handle non-finite values.
Results may differ from a plain program's by a relative error of at most 0.012.
Values may be sent and summed in bfloat16 or wider, within the bound.
No kernel may reach another device: no remote copies, remote signals or barrier semaphores. Data moves between devices by JAX's collectives and lax.ppermute only.
A program may use at most 128 MiB of HBM per device.

v0:
```python
import jax
import jax.numpy as jnp
from jax import lax
from jax.sharding import PartitionSpec as P


def expert_rows(tile_in, gate_w, up_w, down_w):
    gate_val = jnp.dot(tile_in, gate_w, preferred_element_type=jnp.float32)
    up_val = jnp.dot(tile_in, up_w, preferred_element_type=jnp.float32)
    hidden = ((up_val + 1.0) * gate_val * jax.nn.sigmoid(1.702 * gate_val)).astype(jnp.bfloat16)
    return jnp.dot(hidden, down_w, preferred_element_type=jnp.float32).astype(jnp.bfloat16)


def run_tiles(packed, first_row, last_row, gate_w, up_w, down_w):
    tile_rows = 128
    n_tiles = jnp.maximum(last_row - first_row + tile_rows - 1, 0) // tile_rows
    result_buf = jnp.zeros((packed.shape[0], down_w.shape[1]), jnp.bfloat16)

    def advance(index_t, buffer):
        at_row = first_row + index_t * tile_rows
        tile_in = lax.dynamic_slice_in_dim(packed, at_row, tile_rows, 0)
        return lax.dynamic_update_slice_in_dim(
            buffer, expert_rows(tile_in, gate_w, up_w, down_w), at_row, 0
        )

    return lax.fori_loop(0, n_tiles, advance, result_buf)


def per_device(tokens, expert_ids, gate_logits, w_gate, w_up, w_down):
    n_rows, width = tokens.shape
    n_tops = expert_ids.shape[1]
    n_exp = lax.axis_size("expert")
    n_dp = lax.axis_size("dp")
    slot_cap = max(2, 3 * n_rows * n_tops // (2 * n_exp))
    tile_rows = 128
    flat_ids = expert_ids.reshape(-1)
    onehot = (flat_ids[:, None] == jnp.arange(n_exp, dtype=jnp.int32)[None, :]).astype(jnp.int32)
    rank_in = jnp.sum((jnp.cumsum(onehot, axis=0) - onehot) * onehot, axis=1)
    counts = jnp.sum(onehot, axis=0)
    slot_idx = flat_ids * slot_cap + rank_in
    source = (
        jnp.zeros((n_exp * slot_cap,), jnp.int32)
        .at[slot_idx]
        .set(jnp.arange(n_rows * n_tops, dtype=jnp.int32) // n_tops)
    )
    filled = (jnp.arange(slot_cap)[None, :] < counts[:, None]).reshape(-1)
    outgoing = jnp.where(filled[:, None], tokens[source], jnp.zeros_like(tokens[source])).reshape(
        n_exp, slot_cap, width
    )
    rows_mid, counts_mid = (
        lax.all_to_all(outgoing, "expert", split_axis=0, concat_axis=0, tiled=True),
        lax.all_to_all(counts[:, None], "expert", split_axis=0, concat_axis=0, tiled=True),
    )
    rows_in, counts_in = (
        lax.all_gather(rows_mid, "dp", axis=0, tiled=True),
        lax.all_gather(counts_mid, "dp", axis=0, tiled=True),
    )
    rows_flat = rows_in.reshape(-1, width)
    total_rows = rows_flat.shape[0]
    live_row = (jnp.arange(slot_cap)[None, :] < counts_in.reshape(-1)[:, None]).reshape(-1)
    position = jnp.cumsum(live_row.astype(jnp.int32)) - 1
    live_total = jnp.sum(live_row.astype(jnp.int32))
    padded = (total_rows + tile_rows - 1) // tile_rows * tile_rows + tile_rows
    gather_idx = (
        jnp.zeros((padded,), jnp.int32)
        .at[jnp.where(live_row, position, padded)]
        .set(jnp.arange(total_rows, dtype=jnp.int32), mode="drop")
    )
    packed = rows_flat[gather_idx]
    gate_w = w_gate[0]
    up_w = w_up[0]
    down_w = w_down[0]
    merged = run_tiles(packed, 0, live_total, gate_w, up_w, down_w)
    slot_out = jnp.where(
        live_row[:, None],
        merged[jnp.where(live_row, position, 0)],
        jnp.zeros((total_rows, width), jnp.bfloat16),
    )
    summed = lax.psum_scatter(
        slot_out.reshape(n_dp * n_exp, slot_cap, width), "dp", scatter_dimension=0, tiled=True
    ).astype(jnp.float32)
    expert_out = lax.all_to_all(
        summed.astype(jnp.bfloat16), "expert", split_axis=0, concat_axis=0, tiled=True
    )
    picked = expert_out.reshape(n_exp * slot_cap, width)[slot_idx]
    gate_wts = jnp.exp(gate_logits)
    gate_wts = gate_wts / jnp.sum(gate_wts, axis=1, keepdims=True)
    mixed = jnp.sum(
        picked.reshape(n_rows, n_tops, width).astype(jnp.float32) * gate_wts[:, :, None], axis=1
    )
    return mixed.astype(jnp.bfloat16)


def solution(mesh):
    return jax.shard_map(
        per_device,
        mesh=mesh,
        in_specs=(
            P(("expert", "dp"), None),
            P(("expert", "dp"), None),
            P(("expert", "dp"), None),
            P("expert", None, "dp"),
            P("expert", None, "dp"),
            P("expert", "dp", None),
        ),
        out_specs=P(("expert", "dp"), None),
        check_vma=False,
    )
```

profile of v0, /device:TPU:8, one launch (start us, length us, event | category | flops | bytes accessed | tf_op | source)
XLA Modules:
  0.0 598.1 jit_solution(584529033476823874)
XLA Ops:
  17.6 82.8 %all_to_all.22 = bf16[64,6,2880]{2,1,0:T(8,128)(2,1)S(1)} all-to-all(bf16[64,6,2880]{2,1,0:T(8,128)(2,1)S(1)} %broadcast_select_fusion.1), channel_id=1, replica_groups=mesh['expert'=64,'dp'=4] {'expert'}, dimensions={0} | all-to-all | bytes 4423680 | tf_op jit(solution)/shard_map/all_to_all | solution.py:51
  102.8 5.7 all-to-all-start
  112.9 4.2 all-to-all-done
  118.6 9.3 %all-reduce = s32[256]{0:T(256)S(1)} all-reduce(s32[256]{0:T(256)S(1)} %dynamic-update-slice), channel_id=2, replica_groups=mesh['expert'=64,'dp'=4] {'dp'}, use_global_device_ids=true, to_apply=%add | all-reduce | flops 256 | bytes 2048
  130.3 6.4 %scatter_custom_fusion.1 = s32[1664]{0:T(1024)S(1)} fusion(s32[1536]{0:T(1024)S(1)} %get-tuple-element.45, s32[1536]{0:T(1024)S(1)} %iota.22, s32[]{:T(128)} %constant.65.clone.1), kind=kCustom, calls=%fused_computation.57 | custom fusion | bytes 6660 | tf_op jit(solution)/shard_map/scatter | solution.py:67
  136.8 53.3 %all-gather.3.cloned.1.call-done = bf16[256,6,2880]{2,0,1:T(8,128)(2,1)} async-done(((bf16[64,6,2880]{2,0,1:T(8,128)(2,1)}), bf16[256,6,2880]{2,0,1:T(8,128)(2,1)}) %all-gather.3.cloned.1.call-update) | async-done | bytes 8847376 | tf_op jit(solution)/shard_map/all_gather | solution.py:55
  190.1 12.9 %copy.33 = bf16[256,6,2880]{2,1,0:T(8,128)(2,1)} copy(bf16[256,6,2880]{2,0,1:T(8,128)(2,1)} %all-gather.3.cloned.1.call-done) | data formatting | bytes 17694720 | tf_op jit(solution)/shard_map/all_gather | solution.py:55
  203.0 15.1 %reshape.195 = bf16[1536,2880]{1,0:T(8,128)(2,1)} reshape(bf16[256,6,2880]{2,1,0:T(8,128)(2,1)} %copy.33) | data formatting | bytes 17694720 | tf_op jit(solution)/shard_map/reshape | solution.py:58
  218.1 24.0 %gather_fusion.1 = bf16[1664,2880]{1,0:T(8,128)(2,1)} fusion(bf16[1536,2880]{1,0:T(8,128)(2,1)} %reshape.195, s32[2048]{0:T(1024)S(1)} %pad_clamp_fusion.1), kind=kCustom, calls=%fused_computation.1 | custom fusion | bytes 19175936 | tf_op jit(solution)/shard_map/gather | solution.py:69
  242.1 4.3 broadcast_in_dim.48
  246.4 78.7 %while.10 = (s32[]{:T(128)}, bf16[1664,2880]{0,1:T(8,128)(2,1)}, s32[]{:T(128)}, bf16[1664,2880]{1,0:T(8,128)(2,1)}, bf16[2880,384]{1,0:T(8,128)(2,1)}, /*index=...) while((s32[]{:T(128)}, bf16[1664,2880]{0,1:T(8,128)(2,1)}, ...), condition=%wide.region_10.11_spmd, body=%wide.region_9.10_spmd.sunk | while | flops 850108416 | bytes 9274527 | solution.py:26
  248.8 4.1 fusion.46
  255.4 4.2 fusion.46
  268.5 4.2 fusion.46
  294.7 4.2 fusion.46
  307.9 4.2 fusion.46
  321.0 4.2 fusion.46
  325.2 14.0 %copy.35 = bf16[1664,2880]{1,0:T(8,128)(2,1)} copy(bf16[1664,2880]{0,1:T(8,128)(2,1)} %get-tuple-element.43) | data formatting | bytes 19169280 | tf_op jit(solution)/shard_map/while | solution.py:26
  339.2 21.9 %gather_fusion.2 = bf16[1536,2880]{1,0:T(8,128)(2,1)} fusion(bf16[1664,2880]{1,0:T(8,128)(2,1)} %copy.35, s32[2048]{0:T(1024)S(1)} %pad_clamp_fusion), kind=kCustom, calls=%fused_computation.2 | custom fusion | bytes 17700864 | tf_op jit(solution)/shard_map/gather | solution.py:76
  361.1 13.9 %gather.20 = bf16[256,6,2880]{2,1,0:T(8,128)(2,1)} reshape(bf16[1536,2880]{1,0:T(8,128)(2,1)} %gather_fusion.2) | data formatting | bytes 17694720 | tf_op jit(solution)/shard_map/gather | solution.py:76
  375.0 10.6 %broadcast_select_fusion = bf16[256,6,2880]{2,1,0:T(8,128)(2,1)} fusion(bf16[256,6,2880]{2,1,0:T(8,128)(2,1)} %gather.20, pred[256,6]{1,0:T(8,128)(4,1)S(1)} %get-tuple-element.63), kind=kLoop, calls=%fused_computation.26 | loop fusion | flops 4423680 | bytes 17696256 | tf_op jit(solution)/shard_map/jit(_where)/select_n | solution.py:74
  385.7 112.4 %reduce-scatter.2.cloned.1.call-done = bf16[64,6,2880]{2,1,0:T(8,128)(2,1)} async-done(((bf16[256,6,2880]{2,1,0:T(8,128)(2,1)}), bf16[64,6,2880]{2,1,0:T(8,128)(2,1)}) %reduce-scatter.2.cloned.1.call-update) | async-done | bytes 2211856 | tf_op jit(solution)/shard_map/reduce_scatter | solution.py:79
  498.1 10.7 %all-to-all-start.2 = ((bf16[64,6,2880]{2,1,0:T(8,128)(2,1)}), bf16[64,6,2880]{2,1,0:T(8,128)(2,1)}, u32[]{:S(2)}, u32[]{:S(2)}) async-start(bf16[64,6,2880]{2,1,0:T(8,128)(2,1)} %reduce-scatter.2.cloned.1.call-done), calls=%async_computation.3 | async-start | bytes 6029312 | tf_op jit(solution)/shard_map/all_to_all | solution.py:82
  509.0 70.7 %all-to-all-done.2 = bf16[64,6,2880]{2,1,0:T(8,128)(2,1)} async-done(((bf16[64,6,2880]{2,1,0:T(8,128)(2,1)}), bf16[64,6,2880]{2,1,0:T(8,128)(2,1)}, u32[]{:S(2)}, u32[]{:S(2)}) %all-to-all-start.2) | async-done | bytes 2211872 | tf_op jit(solution)/shard_map/all_to_all | solution.py:82
  (80 shorter events, 85.8 us)
Async XLA Ops:
  6.5 4.4 copy-start
  6.5 183.6 %all-gather.3.cloned.1.call-start = ((), (), s32[]{:S(2)}) async-start(), calls=%async_computation.4 | async-start | bytes 11304960 | tf_op jit(solution)/shard_map/all_gather | solution.py:55
  102.1 9.6 %copy-start.3 = (u32[256]{0:T(256)S(1)}, u32[256]{0:T(256)}, u32[]{:S(2)}) copy-start(u32[256]{0:T(256)} %constant.87) | copy-start | bytes 3076
  102.8 14.3 %all-to-all-start = ((s32[64,1,1]{2,1,0:T(1,128)}), s32[64,1,1]{2,1,0:T(1,128)S(1)}, u32[]{:S(2)}, u32[]{:S(2)}) async-start(s32[64,1,1]{2,1,0:T(1,128)} %copy.28), calls=%async_computation | async-start | bytes 65536 | tf_op jit(solution)/shard_map/all_to_all | solution.py:52
  108.6 389.6 %reduce-scatter.2.cloned.1.call-start = ((), (), s32[]{:S(2)}) async-start(), calls=%async_computation.5 | async-start | bytes 15073280 | tf_op jit(solution)/shard_map/reduce_scatter | solution.py:79
  385.7 123.2 %copy-start.2 = (f32[64,4]{0,1:T(4,128)S(1)}, f32[64,4]{0,1:T(4,128)}, u32[]{:S(2)}) copy-start(f32[64,4]{0,1:T(4,128)} %param.10) | copy-start | bytes 3076
  498.1 81.6 %all-to-all-start.2 = ((bf16[64,6,2880]{2,1,0:T(8,128)(2,1)}), bf16[64,6,2880]{2,1,0:T(8,128)(2,1)}, u32[]{:S(2)}, u32[]{:S(2)}) async-start(bf16[64,6,2880]{2,1,0:T(8,128)(2,1)} %reduce-scatter.2.cloned.1.call-done), calls=%async_computation.3 | async-start | bytes 6029312 | tf_op jit(solution)/shard_map/all_to_all | solution.py:82
  583.0 8.3 %copy-start.1 = (bf16[64,2880]{1,0:T(8,128)(2,1)S(1)}, bf16[64,2880]{1,0:T(8,128)(2,1)}, u32[]{:S(2)}) copy-start(bf16[64,2880]{1,0:T(8,128)(2,1)} %param.8) | copy-start | bytes 1105924
Sparse Core Ops, SparseCore 0:
  102.3 87.7 all-gather.2
  385.8 112.2 reduce-scatter.1
where the time goes:
time: 602 us; the launch traced here: 598 us
  waiting for transfers between devices  241 us (40%)
  local copies, waits for them, and re-layouts  137 us (23%)
  blocking collectives  92.1 us (15%)
  matrix products  78.6 us (13%)
  other arithmetic  17.9 us (3%)
  starting transfers between devices  16.5 us (3%)
  between operations  15 us (2%)
    reduce_scatter x1, waiting for transfers between devices, per_device(): lax.psum_scatter(slot_out.reshape(n_dp * n_exp, slot_cap, width), 'dp', s...  112 us
    all_to_all x1, blocking collectives, per_device(): lax.all_to_all(outgoing, 'expert', split_axis=0, concat_axis=0, tiled=True)  82.8 us
    all_to_all x1, waiting for transfers between devices, per_device(): lax.all_to_all(summed.astype(jnp.bfloat16), 'expert', split_axis=0, conca...  70.7 us
    all_gather x1, waiting for transfers between devices, per_device(): lax.all_gather(rows_mid, 'dp', axis=0, tiled=True)  53.3 us
    dot_general x12, matrix products, expert_rows(): jnp.dot(hidden, down_w, preferred_element_type=jnp.float32)  49.8 us
    gather x2, local copies, waits for them, and re-layouts, per_device(): merged[jnp.where(live_row, position, 0)]  35.8 us
    dot_general x12, matrix products, expert_rows(): gate_val = jnp.dot(tile_in, gate_w, preferred_element_type=jnp.float32)  28.9 us
    gather x1, local copies, waits for them, and re-layouts, per_device(): packed = rows_flat[gather_idx]  24 us
  transfers between devices with their start and end apart: 4, of which 4 were waited for; matrix products, arithmetic and copies ran while one was open for 2% of the time, Pallas kernels for 0%

commit v1 on v0

v1 whole, which is shorter than its diff:
```python
import jax
import jax.numpy as jnp
from jax import lax
from jax.experimental import pallas as pl
from jax.sharding import PartitionSpec as P

CHUNKS = (2, 2, 2)
SPLIT = "hPP"
CUT = (0, 2880)
PAIRS = {"P": ((0, 1), (1, 0), (2, 3), (3, 2)), "A": ((0, 3), (3, 0), (1, 2), (2, 1))}
F32, BF16 = jnp.float32, jnp.bfloat16


def rows_of(ref):
    return [ref[...]] if len(ref.shape) == 2 else [ref[i] for i in range(ref.shape[0])]


def hidden_body(*refs):
    ins, (gate_w, up_w, send, keep) = refs[:-4], refs[-4:]
    rows = jnp.concatenate([piece for ref in ins for piece in rows_of(ref)], axis=0)
    gate = jnp.dot(rows, gate_w[...], preferred_element_type=F32)
    up = jnp.dot(rows, up_w[...], preferred_element_type=F32)
    hidden = ((up + 1.0) * gate * jax.nn.sigmoid(1.702 * gate)).astype(BF16)
    half = send.shape[0]
    send[...] = hidden[:half]
    keep[...] = hidden[half:]


def hidden_rows(ins, gate_w, up_w):
    _, half, width = ins[0].shape
    units = gate_w.shape[1]
    return pl.pallas_call(
        hidden_body,
        out_shape=[jax.ShapeDtypeStruct((4 * half, units), BF16)] * 2,
        name="hidden",
        cost_estimate=pl.CostEstimate(flops=32 * half * width * units, transcendentals=8 * half * units, bytes_accessed=8 << 20),
    )(*ins, gate_w, up_w)


def down_body(keep, recv, own_w, *refs):
    pieces, (own, adjacent) = refs[:-2], refs[-2:]
    nt = (((1,), (1,)), ((), ()))
    half = own.shape[1]
    at = 0
    for piece in pieces:
        end = at + piece.shape[0]
        total = lax.dot_general(keep[...], own_w[at:end], nt, preferred_element_type=F32)
        total += lax.dot_general(recv[...], piece[...], nt, preferred_element_type=F32)
        total = total.astype(BF16)
        for index, ref in enumerate((own, adjacent)):
            for side in range(2):
                row = (2 * index + side) * half
                ref[side, :, at:end] = total[row:row + half]
        at = end


def down_rows(keep, recv, own_w, pieces):
    rows = keep.shape[0]
    width, units = own_w.shape
    pair = jax.ShapeDtypeStruct((2, rows // 4, width), BF16)
    return pl.pallas_call(
        down_body,
        out_shape=[pair, pair],
        name="down",
        cost_estimate=pl.CostEstimate(flops=4 * rows * width * units, transcendentals=0, bytes_accessed=6 << 20),
    )(keep, recv, own_w, *pieces)


def layer(tokens, expert_ids, gate_logits, w_gate, w_up, w_down):
    n_rows, width = tokens.shape
    n_exp = lax.axis_size("expert")

    def send(value, way):
        return lax.ppermute(value, "dp", PAIRS[way])

    def exchange(value):
        return lax.all_to_all(value, "expert", split_axis=0, concat_axis=0, tiled=True)

    named = expert_ids[None, :, :] == jnp.arange(n_exp, dtype=jnp.int32)[:, None, None]
    member = jnp.any(named, axis=2)
    tri = (jnp.arange(n_rows)[:, None] < jnp.arange(n_rows)[None, :]).astype(BF16)
    rank = jnp.dot(member.astype(BF16), tri, preferred_element_type=F32)
    weights = jnp.exp(gate_logits)
    weights = weights / jnp.sum(weights, axis=1, keepdims=True)
    by_expert = jnp.sum(jnp.where(named, weights[None], 0.0), axis=2)
    gate_w, up_w, own_w = w_gate[0], w_up[0], w_down[0].T
    pieces = []
    for lo, hi in zip(CUT, CUT[1:]):
        cut = own_w[lo:hi]
        pieces.append(send(cut, "P"))

    base = 0
    rows_out = []
    for c, size in enumerate(CHUNKS):
        slots = base + jnp.arange(size, dtype=jnp.int32).astype(F32)
        onehot = (member[:, None, :] & (rank[:, None, :] == slots[None, :, None]))
        onehot = onehot.reshape(n_exp * size, n_rows)
        sent = jnp.dot(onehot.astype(BF16), tokens, preferred_element_type=F32).astype(BF16)
        sent = sent.reshape(n_exp, size, width)
        mid = exchange(sent)
        own = mid.reshape(2, n_exp * size // 2, width)
        partner = send(own, "P")
        adjacent = send(own, "A")
        if SPLIT[c] == "h":
            far = [send(partner[0], "A"), send(adjacent[1], "P")]
        elif SPLIT[c] == "A":
            far = [send(partner, "A")]
        else:
            far = [send(adjacent, "P")]
        away, keep = hidden_rows([partner, *far, own, adjacent], gate_w, up_w)
        recv = send(away, "P")
        mine, theirs = down_rows(keep, recv, own_w, pieces)
        other = send(theirs, "A")
        summed = (mine.astype(F32) + other.astype(F32)).astype(BF16).reshape(n_exp, size, width)
        back = exchange(summed).reshape(n_exp * size, width)
        scale = jnp.where(onehot.reshape(n_exp, size, n_rows), by_expert[:, None, :], 0.0).reshape(n_exp * size, n_rows)
        high = scale.astype(BF16)
        low = (scale - high.astype(F32)).astype(BF16)
        dims = (((0,), (0,)), ((), ()))
        rows_out.append(
            lax.dot_general(high, back, dims, preferred_element_type=F32)
            + lax.dot_general(low, back, dims, preferred_element_type=F32)
        )
        base += size
    return sum(rows_out).astype(BF16)


def solution(mesh):
    return jax.shard_map(
        layer,
        mesh=mesh,
        in_specs=(
            P(("expert", "dp"), None),
            P(("expert", "dp"), None),
            P(("expert", "dp"), None),
            P("expert", None, "dp"),
            P("expert", None, "dp"),
            P("expert", "dp", None),
        ),
        out_specs=P(("expert", "dp"), None),
        check_vma=False,
    )
```

time: 602 us -> 299 us (0.50)
  local copies, waits for them, and re-layouts: 137 us -> 26.8 us
  blocking collectives: 92.1 us -> 0 us
  waiting for transfers between devices: 241 us -> 151 us
  matrix products: 78.6 us -> 4.9 us
  starting transfers between devices: 16.5 us -> 70.7 us
  Pallas kernels: 0 us -> 38.4 us
  between operations: 15 us -> 0.27 us
  other arithmetic: 17.9 us -> 4.69 us
    reduce_scatter x1 -> x0, waiting for transfers between devices: 112 us -> none  [per_device(): lax.psum_scatter(slot_out.reshape(n_dp * n_exp, slot_cap, width), 'dp', s...]
    ppermute x0 -> x17, waiting for transfers between devices: none -> 87.6 us  [send(): return lax.ppermute(value, 'dp', PAIRS[way])]
    all_to_all x1 -> x0, blocking collectives: 82.8 us -> none  [per_device(): lax.all_to_all(outgoing, 'expert', split_axis=0, concat_axis=0, tiled=True)]
    dot_general x24 -> x10, matrix products: 78.6 us -> 4.9 us  [the longest x3 2.23 us: layer(): jnp.dot(onehot.astype(BF16), tokens, preferred_element_type=F32)]
    gather x6 -> x0, local copies, waits for them, and re-layouts: 68.7 us -> none  [the longest x2 35.8 us: per_device(): merged[jnp.where(live_row, position, 0)]]
    all_gather x1 -> x0, waiting for transfers between devices: 53.3 us -> none  [per_device(): lax.all_gather(rows_mid, 'dp', axis=0, tiled=True)]
    pallas_call x0 -> x6, Pallas kernels: none -> 38.4 us  [the longest x3 21.9 us: hidden_rows(): pl.pallas_call(hidden_body, out_shape=[jax.ShapeDtypeStruct((4 * half, un...]
    all_to_all x2 -> x6, starting transfers between devices: 16.4 us -> 50 us  [exchange(): lax.all_to_all(value, 'expert', split_axis=0, concat_axis=0, tiled=True)]
  transfers between devices with their start and end apart: 4 -> 23, of which waited for: 4 -> 12; matrix products, arithmetic and copies ran while one was open for 2% -> 9% of each run, Pallas kernels for 0% -> 13%
where the time goes in v1:
time: 299 us; the launch traced here: 297 us
  waiting for transfers between devices  151 us (51%)
  starting transfers between devices  70.7 us (24%)
  Pallas kernels  38.4 us (13%)
  local copies, waits for them, and re-layouts  26.8 us (9%)
  matrix products  4.9 us (2%)
  other arithmetic  4.69 us (2%)
    ppermute x17, waiting for transfers between devices, send(): return lax.ppermute(value, 'dp', PAIRS[way])  87.6 us
    all_to_all x6, waiting for transfers between devices, exchange(): lax.all_to_all(value, 'expert', split_axis=0, concat_axis=0, tiled=True)  63.3 us
    all_to_all x6, starting transfers between devices, exchange(): lax.all_to_all(value, 'expert', split_axis=0, concat_axis=0, tiled=True)  50 us
    pallas_call x3, Pallas kernels, hidden_rows(): pl.pallas_call(hidden_body, out_shape=[jax.ShapeDtypeStruct((4 * half, un...  21.9 us
    ppermute x17, starting transfers between devices, send(): return lax.ppermute(value, 'dp', PAIRS[way])  20.7 us
    pallas_call x3, Pallas kernels, down_rows(): pl.pallas_call(down_body, out_shape=[pair, pair], name='down', cost_estim...  16.6 us
    reshape x3, local copies, waits for them, and re-layouts, layer(): own = mid.reshape(2, n_exp * size // 2, width)  7.25 us
  transfers between devices with their start and end apart: 23, of which 12 were waited for; matrix products, arithmetic and copies ran while one was open for 9% of the time, Pallas kernels for 13%

profile of v1, /device:TPU:8, one launch (start us, length us, event | category | flops | bytes accessed | tf_op | source)
XLA Modules:
  0.0 296.8 jit_solution(5418157664009016229)
XLA Ops:
  3.2 12.1 %all-to-all-start = ((bf16[64,2,2880]{2,1,0:T(2,128)(2,1)}), bf16[64,2,2880]{2,1,0:T(2,128)(2,1)S(1)}, u32[]{:S(2)}, u32[]{:S(2)}) async-start(bf16[64,2,2880]{2,1,0:T(2,128)(2,1)} %reshape.109), calls=%async_computation | async-start | bytes 1507328 | tf_op jit(solution)/shard_map/all_to_all | solution.py:77
  17.4 20.3 %all-to-all-done = bf16[64,2,2880]{2,1,0:T(2,128)(2,1)S(1)} async-done(((bf16[64,2,2880]{2,1,0:T(2,128)(2,1)}), bf16[64,2,2880]{2,1,0:T(2,128)(2,1)S(1)}, u32[]{:S(2)}, u32[]{:S(2)}) %all-to-all-start) | async-done | bytes 737312 | tf_op jit(solution)/shard_map/all_to_all | solution.py:77
  38.6 5.8 %all-to-all-start.2 = ((bf16[64,2,2880]{2,1,0:T(2,128)(2,1)}), bf16[64,2,2880]{2,1,0:T(2,128)(2,1)S(1)}, u32[]{:S(2)}, u32[]{:S(2)}) async-start(bf16[64,2,2880]{2,1,0:T(2,128)(2,1)} %reshape.112), calls=%async_computation.2 | async-start | bytes 1507328 | tf_op jit(solution)/shard_map/all_to_all | solution.py:77
  58.7 8.1 %all-to-all-done.2 = bf16[64,2,2880]{2,1,0:T(2,128)(2,1)S(1)} async-done(((bf16[64,2,2880]{2,1,0:T(2,128)(2,1)}), bf16[64,2,2880]{2,1,0:T(2,128)(2,1)S(1)}, u32[]{:S(2)}, u32[]{:S(2)}) %all-to-all-start.2) | async-done | bytes 737312 | tf_op jit(solution)/shard_map/all_to_all | solution.py:77
  67.7 5.8 %all-to-all-start.4 = ((bf16[64,2,2880]{2,1,0:T(2,128)(2,1)}), bf16[64,2,2880]{2,1,0:T(2,128)(2,1)S(1)}, u32[]{:S(2)}, u32[]{:S(2)}) async-start(bf16[64,2,2880]{2,1,0:T(2,128)(2,1)} %reshape.115), calls=%async_computation.4 | async-start | bytes 1507328 | tf_op jit(solution)/shard_map/all_to_all | solution.py:77
  84.1 13.6 %collective-permute-done.8.refs_3_ = bf16[2,64,2880]{2,1,0:T(8,128)(2,1)} collective-permute-done((bf16[2,64,2880]{2,1,0:T(8,128)(2,1)}, bf16[2,64,2880]{2,1,0:T(8,128)(2,1)}, u32[]{:S(2)}, u32[]{:S(2)}) %collective-permute-start.8) | collective-permute-done | bytes 737312 | tf_op jit(solution)/shard_map/ppermute | solution.py:74
  97.9 6.8 %collective-permute-done.1.refs_1_ = bf16[64,2880]{1,0:T(8,128)(2,1)S(1)} collective-permute-done((bf16[64,2880]{1,0:T(8,128)(2,1)S(1)}, bf16[64,2880]{1,0:T(8,128)(2,1)S(1)}, u32[]{:S(2)}, u32[]{:S(2)}) %collective-permute-start.1) | collective-permute-done | bytes 368672 | tf_op jit(solution)/shard_map/ppermute | solution.py:74
  104.8 17.9 %collective-permute-done.3.refs_2_ = bf16[64,2880]{1,0:T(8,128)(2,1)S(1)} collective-permute-done((bf16[64,2880]{1,0:T(8,128)(2,1)S(1)}, bf16[64,2880]{1,0:T(8,128)(2,1)S(1)}, u32[]{:S(2)}, u32[]{:S(2)}) %collective-permute-start.3) | collective-permute-done | bytes 368672 | tf_op jit(solution)/shard_map/ppermute | solution.py:74
  123.5 7.3 %hidden.3 = (bf16[256,384]{1,0:T(8,128)(2,1)}, bf16[256,384]{1,0:T(8,128)(2,1)}) custom-call(bf16[2,64,2880]{2,1,0:T(8,128)(2,1)} %collective-permute-done.refs_0_, bf16[64,2880]{1,0:T(8,128)(2,1)} %copy-done.14, bf16[64,2880]{1,0:T(8,128)(2,1)} %copy-done.15, bf16[2,64,2880]{2,1,0:T(8,128)(2,1)} %reshape.110.refs_3_, ...), custom_call_target="tpu_custom_call" | custom-call | flops 2264924160 | bytes 8388608 | tf_op jit(solution)/shard_map/hidden/pallas_call | solution.py:32
  135.8 22.7 %collective-permute-done.4.recv = bf16[256,384]{1,0:T(8,128)(2,1)} collective-permute-done((bf16[256,384]{1,0:T(8,128)(2,1)}, bf16[256,384]{1,0:T(8,128)(2,1)}, u32[]{:S(2)}, u32[]{:S(2)}) %collective-permute-start.4) | collective-permute-done | bytes 196640 | tf_op jit(solution)/shard_map/ppermute | solution.py:74
  158.4 5.5 %down.3 = (bf16[2,64,2880]{2,1,0:T(8,128)(2,1)}, bf16[2,64,2880]{2,1,0:T(8,128)(2,1)}) custom-call(bf16[256,384]{1,0:T(8,128)(2,1)} %get-tuple-element.17.keep, bf16[256,384]{1,0:T(8,128)(2,1)} %collective-permute-done.4.recv, bf16[2880,384]{1,0:T(8,128)(2,1)} %bitcast.38, bf16[2880,384]{1,0:T(8,128)(2,1)} %collective-permute-done.5.refs_0_), custom_call_target="tpu_custom_call" | custom-call | flops 1132462080 | bytes 6291456 | tf_op jit(solution)/shard_map/down/pallas_call | solution.py:61
  166.7 7.3 %hidden.4 = (bf16[256,384]{1,0:T(8,128)(2,1)}, bf16[256,384]{1,0:T(8,128)(2,1)}) custom-call(bf16[2,64,2880]{2,1,0:T(8,128)(2,1)} %collective-permute-done.7.refs_0_, bf16[2,64,2880]{2,1,0:T(8,128)(2,1)} %collective-permute-done.9.refs_1_, bf16[2,64,2880]{2,1,0:T(8,128)(2,1)} %reshape.113.refs_2_, bf16[2,64,2880]{2,1,0:T(8,128)(2,1)} %collective-permute-done.8.refs_3_, ...), custom_call_target="tpu_custom_call" | custom-call | flops 2264924160 | bytes 8388608 | tf_op jit(solution)/shard_map/hidden/pallas_call | solution.py:32
  176.4 5.6 %collective-permute-done.10.recv = bf16[256,384]{1,0:T(8,128)(2,1)S(1)} collective-permute-done((bf16[256,384]{1,0:T(8,128)(2,1)}, bf16[256,384]{1,0:T(8,128)(2,1)S(1)}, u32[]{:S(2)}, u32[]{:S(2)}) %collective-permute-start.10) | collective-permute-done | bytes 196640 | tf_op jit(solution)/shard_map/ppermute | solution.py:74
  182.7 5.5 %down.4 = (bf16[2,64,2880]{2,1,0:T(8,128)(2,1)}, bf16[2,64,2880]{2,1,0:T(8,128)(2,1)}) custom-call(bf16[256,384]{1,0:T(8,128)(2,1)} %get-tuple-element.21.keep, bf16[256,384]{1,0:T(8,128)(2,1)} %copy-done.9, bf16[2880,384]{1,0:T(8,128)(2,1)} %bitcast.39, bf16[2880,384]{1,0:T(8,128)(2,1)} %collective-permute-done.5.refs_0_), custom_call_target="tpu_custom_call" | custom-call | flops 1132462080 | bytes 6291456 | tf_op jit(solution)/shard_map/down/pallas_call | solution.py:61
  192.0 10.3 %all-to-all-start.1 = ((bf16[64,2,2880]{2,1,0:T(2,128)(2,1)}), bf16[64,2,2880]{2,1,0:T(2,128)(2,1)S(1)}, u32[]{:S(2)}, u32[]{:S(2)}) async-start(bf16[64,2,2880]{2,1,0:T(2,128)(2,1)} %reshape.111), calls=%async_computation.1 | async-start | bytes 1507328 | tf_op jit(solution)/shard_map/all_to_all | solution.py:77
  202.4 10.1 %collective-permute-done.14.refs_1_ = bf16[2,64,2880]{2,1,0:T(8,128)(2,1)} collective-permute-done((bf16[2,64,2880]{2,1,0:T(8,128)(2,1)}, bf16[2,64,2880]{2,1,0:T(8,128)(2,1)}, u32[]{:S(2)}, u32[]{:S(2)}) %collective-permute-start.14) | collective-permute-done | bytes 737312 | tf_op jit(solution)/shard_map/ppermute | solution.py:74
  212.4 7.3 %hidden.5 = (bf16[256,384]{1,0:T(8,128)(2,1)}, bf16[256,384]{1,0:T(8,128)(2,1)}) custom-call(bf16[2,64,2880]{2,1,0:T(8,128)(2,1)} %collective-permute-done.12.refs_0_, bf16[2,64,2880]{2,1,0:T(8,128)(2,1)} %collective-permute-done.14.refs_1_, bf16[2,64,2880]{2,1,0:T(8,128)(2,1)} %reshape.116.refs_2_, bf16[2,64,2880]{2,1,0:T(8,128)(2,1)} %collective-permute-done.13.refs_3_, ...), custom_call_target="tpu_custom_call" | custom-call | flops 2264924160 | bytes 8388608 | tf_op jit(solution)/shard_map/hidden/pallas_call | solution.py:32
  220.0 5.6 %collective-permute-done.15.recv = bf16[256,384]{1,0:T(8,128)(2,1)S(1)} collective-permute-done((bf16[256,384]{1,0:T(8,128)(2,1)}, bf16[256,384]{1,0:T(8,128)(2,1)S(1)}, u32[]{:S(2)}, u32[]{:S(2)}) %collective-permute-start.15) | collective-permute-done | bytes 196640 | tf_op jit(solution)/shard_map/ppermute | solution.py:74
  226.3 5.5 %down.5 = (bf16[2,64,2880]{2,1,0:T(8,128)(2,1)}, bf16[2,64,2880]{2,1,0:T(8,128)(2,1)}) custom-call(bf16[256,384]{1,0:T(8,128)(2,1)} %get-tuple-element.25.keep, bf16[256,384]{1,0:T(8,128)(2,1)} %copy-done.10, bf16[2880,384]{1,0:T(8,128)(2,1)} %bitcast.40, bf16[2880,384]{1,0:T(8,128)(2,1)} %collective-permute-done.5.refs_0_), custom_call_target="tpu_custom_call" | custom-call | flops 1132462080 | bytes 6291456 | tf_op jit(solution)/shard_map/down/pallas_call | solution.py:61
  233.7 10.3 %all-to-all-start.3 = ((bf16[64,2,2880]{2,1,0:T(2,128)(2,1)}), bf16[64,2,2880]{2,1,0:T(2,128)(2,1)S(1)}, u32[]{:S(2)}, u32[]{:S(2)}) async-start(bf16[64,2,2880]{2,1,0:T(2,128)(2,1)} %reshape.114), calls=%async_computation.3 | async-start | bytes 1507328 | tf_op jit(solution)/shard_map/all_to_all | solution.py:77
  244.0 5.4 %collective-permute-done.16 = bf16[2,64,2880]{2,1,0:T(8,128)(2,1)} collective-permute-done((bf16[2,64,2880]{2,1,0:T(8,128)(2,1)}, bf16[2,64,2880]{2,1,0:T(8,128)(2,1)}, u32[]{:S(2)}, u32[]{:S(2)}) %collective-permute-start.16) | collective-permute-done | bytes 737312 | tf_op jit(solution)/shard_map/ppermute | solution.py:74
  251.8 14.6 %all-to-all-done.3 = bf16[64,2,2880]{2,1,0:T(2,128)(2,1)S(1)} async-done(((bf16[64,2,2880]{2,1,0:T(2,128)(2,1)}), bf16[64,2,2880]{2,1,0:T(2,128)(2,1)S(1)}, u32[]{:S(2)}, u32[]{:S(2)}) %all-to-all-start.3) | async-done | bytes 737312 | tf_op jit(solution)/shard_map/all_to_all | solution.py:77
  266.4 5.8 %all-to-all-start.5 = ((bf16[64,2,2880]{2,1,0:T(2,128)(2,1)}), bf16[64,2,2880]{2,1,0:T(2,128)(2,1)S(1)}, u32[]{:S(2)}, u32[]{:S(2)}) async-start(bf16[64,2,2880]{2,1,0:T(2,128)(2,1)} %reshape.117), calls=%async_computation.5 | async-start | bytes 1507328 | tf_op jit(solution)/shard_map/all_to_all | solution.py:77
  274.3 20.3 %all-to-all-done.5 = bf16[64,2,2880]{2,1,0:T(2,128)(2,1)S(1)} async-done(((bf16[64,2,2880]{2,1,0:T(2,128)(2,1)}), bf16[64,2,2880]{2,1,0:T(2,128)(2,1)S(1)}, u32[]{:S(2)}, u32[]{:S(2)}) %all-to-all-start.5) | async-done | bytes 737312 | tf_op jit(solution)/shard_map/all_to_all | solution.py:77
  (104 shorter events, 57.1 us)
Async XLA Ops:
  3.2 34.6 %all-to-all-start = ((bf16[64,2,2880]{2,1,0:T(2,128)(2,1)}), bf16[64,2,2880]{2,1,0:T(2,128)(2,1)S(1)}, u32[]{:S(2)}, u32[]{:S(2)}) async-start(bf16[64,2,2880]{2,1,0:T(2,128)(2,1)} %reshape.109), calls=%async_computation | async-start | bytes 1507328 | tf_op jit(solution)/shard_map/all_to_all | solution.py:77
  17.4 31.3 %copy-start.1 = (bf16[1,384,2880]{1,2,0:T(8,128)(2,1)S(1)}, bf16[1,384,2880]{1,2,0:T(8,128)(2,1)}, u32[]{:S(2)}) copy-start(bf16[1,384,2880]{1,2,0:T(8,128)(2,1)} %param.11) | copy-start | bytes 6635524
  38.6 28.2 %all-to-all-start.2 = ((bf16[64,2,2880]{2,1,0:T(2,128)(2,1)}), bf16[64,2,2880]{2,1,0:T(2,128)(2,1)S(1)}, u32[]{:S(2)}, u32[]{:S(2)}) async-start(bf16[64,2,2880]{2,1,0:T(2,128)(2,1)} %reshape.112), calls=%async_computation.2 | async-start | bytes 1507328 | tf_op jit(solution)/shard_map/all_to_all | solution.py:77
  47.3 31.9 %collective-permute-start = (bf16[2,64,2880]{2,1,0:T(8,128)(2,1)}, bf16[2,64,2880]{2,1,0:T(8,128)(2,1)}, u32[]{:S(2)}, u32[]{:S(2)}) collective-permute-start(bf16[2,64,2880]{2,1,0:T(8,128)(2,1)} %reshape.110.refs_3_), channel_id=1, source_target_pairs={{0,1},{1,0},{2,3},{3,2},{4,5},{5,4},{6,7},{7,6},{8,9},{9,8},{10,11... | collective-permute-start | bytes 2211848 | tf_op jit(solution)/shard_map/ppermute | solution.py:74
  48.8 87.0 %collective-permute-start.5 = (bf16[2880,384]{1,0:T(8,128)(2,1)S(1)}, bf16[2880,384]{1,0:T(8,128)(2,1)}, u32[]{:S(2)}, u32[]{:S(2)}) collective-permute-start(bf16[2880,384]{1,0:T(8,128)(2,1)S(1)} %bitcast.41), channel_id=1, source_target_pairs={{0,1},{1,0},{2,3},{3,2},{4,5},{5,4},{6,7},{7,6},{8,9},{9,8},{10,11... | collective-permute-start | bytes 6635528 | tf_op jit(solution)/shard_map/ppermute | solution.py:74
  49.4 31.5 %collective-permute-start.2 = (bf16[2,64,2880]{2,1,0:T(8,128)(2,1)}, bf16[2,64,2880]{2,1,0:T(8,128)(2,1)}, u32[]{:S(2)}, u32[]{:S(2)}) collective-permute-start(bf16[2,64,2880]{2,1,0:T(8,128)(2,1)} %reshape.110.refs_3_), channel_id=1, source_target_pairs={{0,3},{3,0},{1,2},{2,1},{4,7},{7,4},{5,6},{6,5},{8,11},{11,8},{9,1... | collective-permute-start | bytes 2211848 | tf_op jit(solution)/shard_map/ppermute | solution.py:74
  67.7 64.5 %all-to-all-start.4 = ((bf16[64,2,2880]{2,1,0:T(2,128)(2,1)}), bf16[64,2,2880]{2,1,0:T(2,128)(2,1)S(1)}, u32[]{:S(2)}, u32[]{:S(2)}) async-start(bf16[64,2,2880]{2,1,0:T(2,128)(2,1)} %reshape.115), calls=%async_computation.4 | async-start | bytes 1507328 | tf_op jit(solution)/shard_map/all_to_all | solution.py:77
  76.4 21.2 %collective-permute-start.8 = (bf16[2,64,2880]{2,1,0:T(8,128)(2,1)}, bf16[2,64,2880]{2,1,0:T(8,128)(2,1)}, u32[]{:S(2)}, u32[]{:S(2)}) collective-permute-start(bf16[2,64,2880]{2,1,0:T(8,128)(2,1)} %reshape.113.refs_2_), channel_id=1, source_target_pairs={{0,3},{3,0},{1,2},{2,1},{4,7},{7,4},{5,6},{6,5},{8,11},{11,8},{9,1... | collective-permute-start | bytes 2211848 | tf_op jit(solution)/shard_map/ppermute | solution.py:74
  80.2 24.6 %collective-permute-start.1 = (bf16[64,2880]{1,0:T(8,128)(2,1)S(1)}, bf16[64,2880]{1,0:T(8,128)(2,1)S(1)}, u32[]{:S(2)}, u32[]{:S(2)}) collective-permute-start(bf16[64,2880]{1,0:T(8,128)(2,1)S(1)} %slice_bitcast_fusion.1), channel_id=1, source_target_pairs={{0,3},{3,0},{1,2},{2,1},{4,7},{7,4},{5,6},{6,5},{8,11},{11,8},{9,1... | collective-permute-start | bytes 1105928 | tf_op jit(solution)/shard_map/ppermute | solution.py:74
  82.0 40.7 %collective-permute-start.3 = (bf16[64,2880]{1,0:T(8,128)(2,1)S(1)}, bf16[64,2880]{1,0:T(8,128)(2,1)S(1)}, u32[]{:S(2)}, u32[]{:S(2)}) collective-permute-start(bf16[64,2880]{1,0:T(8,128)(2,1)S(1)} %slice_bitcast_fusion), channel_id=1, source_target_pairs={{0,1},{1,0},{2,3},{3,2},{4,5},{5,4},{6,7},{7,6},{8,9},{9,8},{10,11... | collective-permute-start | bytes 1105928 | tf_op jit(solution)/shard_map/ppermute | solution.py:74
  82.3 84.4 %collective-permute-start.7 = (bf16[2,64,2880]{2,1,0:T(8,128)(2,1)}, bf16[2,64,2880]{2,1,0:T(8,128)(2,1)}, u32[]{:S(2)}, u32[]{:S(2)}) collective-permute-start(bf16[2,64,2880]{2,1,0:T(8,128)(2,1)} %reshape.113.refs_2_), channel_id=1, source_target_pairs={{0,1},{1,0},{2,3},{3,2},{4,5},{5,4},{6,7},{7,6},{8,9},{9,8},{10,11... | collective-permute-start | bytes 2211848 | tf_op jit(solution)/shard_map/ppermute | solution.py:74
  97.7 69.1 %collective-permute-start.9 = (bf16[2,64,2880]{2,1,0:T(8,128)(2,1)}, bf16[2,64,2880]{2,1,0:T(8,128)(2,1)}, u32[]{:S(2)}, u32[]{:S(2)}) collective-permute-start(bf16[2,64,2880]{2,1,0:T(8,128)(2,1)} %collective-permute-done.8.refs_3_), channel_id=1, source_target_pairs={{0,1},{1,0},{2,3},{3,2},{4,5},{5,4},{6,7},{7,6},{8,9},{9,8},{10,11... | collective-permute-start | bytes 2211848 | tf_op jit(solution)/shard_map/ppermute | solution.py:74
  130.7 27.7 %collective-permute-start.4 = (bf16[256,384]{1,0:T(8,128)(2,1)}, bf16[256,384]{1,0:T(8,128)(2,1)}, u32[]{:S(2)}, u32[]{:S(2)}) collective-permute-start(bf16[256,384]{1,0:T(8,128)(2,1)} %get-tuple-element.18), channel_id=1, source_target_pairs={{0,1},{1,0},{2,3},{3,2},{4,5},{5,4},{6,7},{7,6},{8,9},{9,8},{10,11... | collective-permute-start | bytes 589832 | tf_op jit(solution)/shard_map/ppermute | solution.py:74
  133.7 42.4 %collective-permute-start.13 = (bf16[2,64,2880]{2,1,0:T(8,128)(2,1)}, bf16[2,64,2880]{2,1,0:T(8,128)(2,1)}, u32[]{:S(2)}, u32[]{:S(2)}) collective-permute-start(bf16[2,64,2880]{2,1,0:T(8,128)(2,1)} %reshape.116.refs_2_), channel_id=1, source_target_pairs={{0,3},{3,0},{1,2},{2,1},{4,7},{7,4},{5,6},{6,5},{8,11},{11,8},{9,1... | collective-permute-start | bytes 2211848 | tf_op jit(solution)/shard_map/ppermute | solution.py:74
  164.0 24.7 %collective-permute-start.6 = (bf16[2,64,2880]{2,1,0:T(8,128)(2,1)}, bf16[2,64,2880]{2,1,0:T(8,128)(2,1)S(1)}, u32[]{:S(2)}, u32[]{:S(2)}) collective-permute-start(bf16[2,64,2880]{2,1,0:T(8,128)(2,1)} %get-tuple-element.20), channel_id=1, source_target_pairs={{0,3},{3,0},{1,2},{2,1},{4,7},{7,4},{5,6},{6,5},{8,11},{11,8},{9,1... | collective-permute-start | bytes 2211848 | tf_op jit(solution)/shard_map/ppermute | solution.py:74
  174.0 8.0 %collective-permute-start.10 = (bf16[256,384]{1,0:T(8,128)(2,1)}, bf16[256,384]{1,0:T(8,128)(2,1)S(1)}, u32[]{:S(2)}, u32[]{:S(2)}) collective-permute-start(bf16[256,384]{1,0:T(8,128)(2,1)} %get-tuple-element.22), channel_id=1, source_target_pairs={{0,1},{1,0},{2,3},{3,2},{4,5},{5,4},{6,7},{7,6},{8,9},{9,8},{10,11... | collective-permute-start | bytes 589832 | tf_op jit(solution)/shard_map/ppermute | solution.py:74
  174.3 28.1 %collective-permute-start.12 = (bf16[2,64,2880]{2,1,0:T(8,128)(2,1)S(1)}, bf16[2,64,2880]{2,1,0:T(8,128)(2,1)}, u32[]{:S(2)}, u32[]{:S(2)}) collective-permute-start(bf16[2,64,2880]{2,1,0:T(8,128)(2,1)S(1)} %copy-done.4), channel_id=1, source_target_pairs={{0,1},{1,0},{2,3},{3,2},{4,5},{5,4},{6,7},{7,6},{8,9},{9,8},{10,11... | collective-permute-start | bytes 2211848 | tf_op jit(solution)/shard_map/ppermute | solution.py:74
  176.1 36.4 %collective-permute-start.14 = (bf16[2,64,2880]{2,1,0:T(8,128)(2,1)}, bf16[2,64,2880]{2,1,0:T(8,128)(2,1)}, u32[]{:S(2)}, u32[]{:S(2)}) collective-permute-start(bf16[2,64,2880]{2,1,0:T(8,128)(2,1)} %collective-permute-done.13.refs_3_), channel_id=1, source_target_pairs={{0,1},{1,0},{2,3},{3,2},{4,5},{5,4},{6,7},{7,6},{8,9},{9,8},{10,11... | collective-permute-start | bytes 2211848 | tf_op jit(solution)/shard_map/ppermute | solution.py:74
  188.2 44.1 %collective-permute-start.11 = (bf16[2,64,2880]{2,1,0:T(8,128)(2,1)}, bf16[2,64,2880]{2,1,0:T(8,128)(2,1)S(1)}, u32[]{:S(2)}, u32[]{:S(2)}) collective-permute-start(bf16[2,64,2880]{2,1,0:T(8,128)(2,1)} %get-tuple-element.24), channel_id=1, source_target_pairs={{0,3},{3,0},{1,2},{2,1},{4,7},{7,4},{5,6},{6,5},{8,11},{11,8},{9,1... | collective-permute-start | bytes 2211848 | tf_op jit(solution)/shard_map/ppermute | solution.py:74
  192.0 41.6 %all-to-all-start.1 = ((bf16[64,2,2880]{2,1,0:T(2,128)(2,1)}), bf16[64,2,2880]{2,1,0:T(2,128)(2,1)S(1)}, u32[]{:S(2)}, u32[]{:S(2)}) async-start(bf16[64,2,2880]{2,1,0:T(2,128)(2,1)} %reshape.111), calls=%async_computation.1 | async-start | bytes 1507328 | tf_op jit(solution)/shard_map/all_to_all | solution.py:77
  219.7 5.9 %collective-permute-start.15 = (bf16[256,384]{1,0:T(8,128)(2,1)}, bf16[256,384]{1,0:T(8,128)(2,1)S(1)}, u32[]{:S(2)}, u32[]{:S(2)}) collective-permute-start(bf16[256,384]{1,0:T(8,128)(2,1)} %get-tuple-element.26), channel_id=1, source_target_pairs={{0,1},{1,0},{2,3},{3,2},{4,5},{5,4},{6,7},{7,6},{8,9},{9,8},{10,11... | collective-permute-start | bytes 589832 | tf_op jit(solution)/shard_map/ppermute | solution.py:74
  231.8 17.5 %collective-permute-start.16 = (bf16[2,64,2880]{2,1,0:T(8,128)(2,1)}, bf16[2,64,2880]{2,1,0:T(8,128)(2,1)}, u32[]{:S(2)}, u32[]{:S(2)}) collective-permute-start(bf16[2,64,2880]{2,1,0:T(8,128)(2,1)} %get-tuple-element.28), channel_id=1, source_target_pairs={{0,3},{3,0},{1,2},{2,1},{4,7},{7,4},{5,6},{6,5},{8,11},{11,8},{9,1... | collective-permute-start | bytes 2211848 | tf_op jit(solution)/shard_map/ppermute | solution.py:74
  233.7 32.8 %all-to-all-start.3 = ((bf16[64,2,2880]{2,1,0:T(2,128)(2,1)}), bf16[64,2,2880]{2,1,0:T(2,128)(2,1)S(1)}, u32[]{:S(2)}, u32[]{:S(2)}) async-start(bf16[64,2,2880]{2,1,0:T(2,128)(2,1)} %reshape.114), calls=%async_computation.3 | async-start | bytes 1507328 | tf_op jit(solution)/shard_map/all_to_all | solution.py:77
  266.4 28.2 %all-to-all-start.5 = ((bf16[64,2,2880]{2,1,0:T(2,128)(2,1)}), bf16[64,2,2880]{2,1,0:T(2,128)(2,1)S(1)}, u32[]{:S(2)}, u32[]{:S(2)}) async-start(bf16[64,2,2880]{2,1,0:T(2,128)(2,1)} %reshape.117), calls=%async_computation.5 | async-start | bytes 1507328 | tf_op jit(solution)/shard_map/all_to_all | solution.py:77
  (15 other events, 107.8 us)
